TPU v7x, 32 devices: a whole 2x2x4 slice. The times are simulated.
32 devices in a mesh: slab: 4 (over y, x), blk: 8 (over z, core).
Axes of the slice: x: 2, y: 2, z: 4, core: 2. Of those that a mesh axis runs over, the one named last changes fastest.
Arguments:
- amplitudes: bfloat16 [32, 3, 56, 128, 128], P('slab', None, 'blk'), may hold values from -6 to 6
- integrals: bfloat16 [32, 3, 1200, 1200], P(('slab', 'blk')), may hold values from -0.03125 to 0.03125
- slot_tile: int32 [56], replicated, may hold values from -1 to 99, as said below
Outputs:
- residual: float32 [3, 56, 128, 128], P(None, 'blk', 'slab')
Inputs may be any that keep to these rules, and one draw needn't show every extreme that they name: `slot_tile`: each of the 55 block pairs x * 10 + y with x <= y is named by exactly one slot; every other slot holds -1.
All inputs are finite; a program needn't handle non-finite values.
Results may differ from a plain program's by a relative error of at most 0.0003.
Values may be sent and summed in bfloat16 or wider, within the bound.
A program may use at most 128 MiB of HBM per device.

v0:
```python
import functools

import jax
import jax.numpy as jnp
from jax import lax
from jax.experimental import pallas as pl
from jax.experimental.pallas import tpu as pltpu
from jax.sharding import PartitionSpec as P


def assemble_kernel(v_width, blocks, slot_ref, packed_ref, full_ref):
    n_blk, _, slot_dev, tile_len, _ = packed_ref.shape
    row_ids = lax.broadcasted_iota(jnp.int32, (tile_len, tile_len), 0)
    col_ids = lax.broadcasted_iota(jnp.int32, (tile_len, tile_len), 1)

    def place(slot, carry):
        tile_id = slot_ref[slot]

        @pl.when(tile_id >= 0)
        def _():
            first = lax.div(tile_id, blocks)
            second = lax.rem(tile_id, blocks)
            rows = pl.ds(pl.multiple_of(first * tile_len, tile_len), tile_len)
            cols = pl.ds(pl.multiple_of(second * tile_len, tile_len), tile_len)
            row_at = row_ids + first * tile_len
            col_at = col_ids + second * tile_len
            keep = jnp.logical_and(row_at < col_at, col_at < v_width)
            packed = packed_ref[lax.div(slot, slot_dev), 0, lax.rem(slot, slot_dev)]
            tile = jnp.where(keep, packed.astype(jnp.float32), 0.0)
            mirror = tile.T

            @pl.when(first == second)
            def _():
                full_ref[rows, cols] = (tile - mirror).astype(full_ref.dtype)

            @pl.when(first != second)
            def _():
                full_ref[rows, cols] = tile.astype(full_ref.dtype)
                full_ref[cols, rows] = (-mirror).astype(full_ref.dtype)

        return carry

    lax.fori_loop(0, n_blk * slot_dev, place, 0)


def assemble(slot_tile, packed, which, v_width, blocks):
    n_blk, _, slot_dev, tile_len, _ = packed.shape
    padded = blocks * tile_len
    return pl.pallas_call(
        functools.partial(assemble_kernel, v_width, blocks),
        grid=(1,),
        out_shape=jax.ShapeDtypeStruct((padded, padded), packed.dtype),
        in_specs=[
            pl.BlockSpec(memory_space=pltpu.SMEM),
            pl.BlockSpec(
                (n_blk, 1, slot_dev, tile_len, tile_len),
                lambda i: (0, which, 0, 0, 0),
                pipeline_mode=pl.Buffered(1),
            ),
        ],
        out_specs=pl.BlockSpec((padded, padded), lambda i: (0, 0), pipeline_mode=pl.Buffered(1)),
        compiler_params=pltpu.CompilerParams(vmem_limit_bytes=24 << 20),
        cost_estimate=pl.CostEstimate(
            flops=0, bytes_accessed=4 * padded * padded, transcendentals=0
        ),
        name="assemble",
    )(slot_tile, packed)


def pair_kernel(
    blocks, n_slab, n_blk, slot_ref, left_ref, right_ref, wl_ref, wr_ref, *rest
):
    out_ref, weights, differ = rest[-3:]
    padded = left_ref.shape[0]
    v_width = wl_ref.shape[-1]
    tile_len = padded // blocks
    row_part = tile_len // n_slab
    slot_dev = out_ref.shape[3]
    pad = padded - v_width
    for half, ref in enumerate((wr_ref, wl_ref)):
        base = half * padded
        vals = ref[0, 0]
        weights[pl.ds(base, v_width), pl.ds(0, v_width)] = vals if half == 0 else -vals
        if pad:
            weights[pl.ds(base, padded), pl.ds(v_width, pad)] = jnp.zeros((padded, pad), weights.dtype)
            weights[pl.ds(base + v_width, pad), :] = jnp.zeros((pad, padded), weights.dtype)

    width = 2 * tile_len if padded % (2 * tile_len) == 0 else tile_len

    def columns(step, carry):
        cols = pl.ds(pl.multiple_of(step * width, width), width)
        top = jnp.dot(left_ref[...], weights[pl.ds(0, padded), cols], preferred_element_type=jnp.float32)
        low = jnp.dot(right_ref[...], weights[pl.ds(padded, padded), cols], preferred_element_type=jnp.float32)
        differ[:, cols] = top + low
        return carry

    lax.fori_loop(0, padded // width, columns, 0)

    def pack(slot, carry):
        tile_id = slot_ref[slot]
        owner = lax.div(slot, slot_dev)
        place = lax.rem(slot, slot_dev)

        @pl.when(tile_id >= 0)
        def _():
            first = lax.div(tile_id, blocks)
            second = lax.rem(tile_id, blocks)
            rows = pl.ds(pl.multiple_of(first * tile_len, tile_len), tile_len)
            cols = pl.ds(pl.multiple_of(second * tile_len, tile_len), tile_len)
            tile = differ[rows, cols] - differ[cols, rows].T
            for slab in range(n_slab):
                part = tile[slab * row_part : (slab + 1) * row_part]
                out_ref[slab, owner, 0, place] = part

        @pl.when(tile_id < 0)
        def _():
            for slab in range(n_slab):
                out_ref[slab, owner, 0, place] = jnp.zeros((row_part, tile_len), jnp.float32)

        return carry

    lax.fori_loop(0, n_blk * slot_dev, pack, 0)


def pair_tiles(slot_tile, fulls, integrals, source, target, pair, n_pair, held, n_slab, n_blk, tile_len):
    padded = fulls[0].shape[0]
    blocks = padded // tile_len
    v_width = integrals.shape[-1]
    slot_dev = slot_tile.shape[0] // n_blk

    def ints(which):
        return pl.BlockSpec((1, 1, v_width, v_width), lambda i: (0, which, 0, 0), pipeline_mode=pl.Buffered(1))

    def whole(shape):
        return pl.BlockSpec(shape, lambda i: (0,) * len(shape), pipeline_mode=pl.Buffered(1))

    row_part = tile_len // n_slab
    out_dims = (n_slab, n_blk, n_pair, slot_dev, row_part, tile_len)
    more = [] if held is None else [held]
    return pl.pallas_call(
        functools.partial(pair_kernel, blocks, n_slab, n_blk),
        grid=(1,),
        out_shape=jax.ShapeDtypeStruct(out_dims, jnp.float32),
        in_specs=[
            pl.BlockSpec(memory_space=pltpu.SMEM),
            whole((padded, padded)),
            whole((padded, padded)),
            ints(source),
            ints(target),
        ]
        + [pl.BlockSpec(memory_space=pl.ANY) for _ in more],
        out_specs=pl.BlockSpec(
            (n_slab, n_blk, 1, slot_dev, row_part, tile_len),
            lambda i: (0, 0, pair, 0, 0, 0),
            pipeline_mode=pl.Buffered(1),
        ),
        input_output_aliases={5: 0} if more else {},
        scratch_shapes=[
            pltpu.VMEM((2 * padded, padded), fulls[0].dtype),
            pltpu.VMEM((padded, padded), jnp.float32),
        ],
        compiler_params=pltpu.CompilerParams(vmem_limit_bytes=56 << 20),
        cost_estimate=pl.CostEstimate(
            flops=4 * padded * padded * padded, bytes_accessed=16 * padded * padded, transcendentals=0
        ),
        name="pair_tiles",
    )(slot_tile, fulls[source], fulls[target], integrals, integrals, *more)


def local(amplitudes, integrals, slot_tile):
    n_slab = lax.axis_size("slab")
    n_blk = lax.axis_size("blk")
    n_out, slot_dev, tile_len = amplitudes.shape[1:4]
    v_width = integrals.shape[-1]
    blocks = (v_width + tile_len - 1) // tile_len
    n_slots = slot_tile.shape[0]
    row_part = tile_len // n_slab
    last = n_out - 1
    head = lax.all_to_all(amplitudes[:, :last], "blk", split_axis=0, concat_axis=0, tiled=True)
    head, rest = lax.optimization_barrier((head, amplitudes[:, last:]))
    tail = lax.all_to_all(rest, "blk", split_axis=0, concat_axis=0, tiled=True)
    fulls = [assemble(slot_tile, head, source, v_width, blocks) for source in range(last)]
    fulls.append(assemble(slot_tile, tail, 0, v_width, blocks))
    pairs = [(source, target) for source in range(n_out) for target in range(source + 1, n_out)]
    held = None
    for source, target in sorted(pairs, key=lambda pair: pair[1]):
        held = pair_tiles(
            slot_tile, fulls, integrals, source, target, pairs.index((source, target)),
            len(pairs), held, n_slab, n_blk, tile_len,
        )
    arranged = held.reshape(n_slab * n_blk, len(pairs), slot_dev, row_part, tile_len)
    share = lax.psum_scatter(arranged, ("slab", "blk"), scatter_dimension=0, tiled=True)
    return share.reshape(len(pairs), slot_dev, row_part, tile_len)


def solution(mesh):
    return jax.shard_map(
        local,
        mesh=mesh,
        in_specs=(P("slab", None, "blk", None, None), P(("slab", "blk"), None, None, None), P()),
        out_specs=P(None, "blk", "slab", None),
        check_vma=False,
    )
```

profile of v0, /device:TPU:0, one launch (start us, length us, event | category | flops | bytes accessed | tf_op | source)
XLA Modules:
  0.0 355.2 jit_solution(1717168203733353506)
XLA Ops:
  6.5 4.4 %slice.6 = bf16[8,2,7,128,128]{4,3,2,1,0:T(8,128)(2,1)} slice(bf16[8,3,7,128,128]{4,3,2,1,0:T(8,128)(2,1)} %param.3), slice={[0:8], [0:2], [0:7], [0:128], [0:128]} | slice | bytes 7340032 | tf_op jit(solution)/shard_map/slice | solution.py:179
  10.9 6.4 %all-to-all-start = ((bf16[8,2,7,128,128]{4,3,2,1,0:T(8,128)(2,1)}), bf16[8,2,7,128,128]{4,3,2,1,0:T(8,128)(2,1)}, u32[]{:S(2)}, u32[]{:S(2)}) async-start(bf16[8,2,7,128,128]{4,3,2,1,0:T(8,128)(2,1)} %slice.6), calls=%async_computation | async-start | bytes 7340032 | tf_op jit(solution)/shard_map/all_to_all | solution.py:179
  17.2 0.0 copy-start.3
  17.3 3.0 slice.7
  20.2 79.8 %all-to-all-done.packed_ref = bf16[8,2,7,128,128]{4,3,2,1,0:T(8,128)(2,1)} async-done(((bf16[8,2,7,128,128]{4,3,2,1,0:T(8,128)(2,1)}), bf16[8,2,7,128,128]{4,3,2,1,0:T(8,128)(2,1)}, u32[]{:S(2)}, u32[]{:S(2)}) %all-to-all-start) | async-done | bytes 3670048 | tf_op jit(solution)/shard_map/all_to_all | solution.py:179
  100.1 3.6 %all-to-all-start.1 = ((bf16[8,1,7,128,128]{4,3,2,1,0:T(8,128)(2,1)}), bf16[8,1,7,128,128]{4,3,2,1,0:T(8,128)(2,1)S(1)}, u32[]{:S(2)}, u32[]{:S(2)}) async-start(bf16[8,1,7,128,128]{4,3,2,1,0:T(8,128)(2,1)} %slice.7), calls=%async_computation.1 | async-start | bytes 3670016 | tf_op jit(solution)/shard_map/all_to_all | solution.py:181
  103.7 0.0 reduce-scatter.2.cloned.1.call-start
  103.7 0.0 copy-done.3
  103.8 8.7 %assemble.5.left_ref = bf16[1280,1280]{1,0:T(8,128)(2,1)S(1)} custom-call(s32[56]{0:T(128)S(1)} %copy-done.3, bf16[8,2,7,128,128]{4,3,2,1,0:T(8,128)(2,1)} %all-to-all-done.packed_ref), custom_call_target="tpu_custom_call" | custom-call | bytes 6553600 | tf_op jit(solution)/shard_map/assemble/pallas_call | solution.py:49
  112.4 0.0 copy-start.1
  112.4 1.6 copy-done.1
  114.1 8.7 %assemble.3.right_ref.left_ref = bf16[1280,1280]{1,0:T(8,128)(2,1)S(1)} custom-call(s32[56]{0:T(128)S(1)} %copy-done.3, bf16[8,2,7,128,128]{4,3,2,1,0:T(8,128)(2,1)} %all-to-all-done.packed_ref), custom_call_target="tpu_custom_call" | custom-call | bytes 6553600 | tf_op jit(solution)/shard_map/assemble/pallas_call | solution.py:49
  122.7 0.0 copy-start
  122.7 1.8 copy-done
  124.5 0.0 copy-start.4
  124.5 23.0 %pair_tiles.3.rest_0_ = f32[4,8,3,7,32,128]{5,4,3,2,1,0:T(8,128)} custom-call(s32[56]{0:T(128)} %slot_ref.11, bf16[1280,1280]{1,0:T(8,128)(2,1)} %copy-done.1, bf16[1280,1280]{1,0:T(8,128)(2,1)} %copy-done, bf16[1,3,1200,1200]{3,2,1,0:T(8,128)(2,1)} %wr_ref.5, bf16[1,3,1200,1200]{3,2,1,0:T(8,128)(2,1)} %wr_ref.5), custom_call_target="tpu_custom_call" | custom-call | flops 8388608000 | bytes 26214400 | tf_op jit(solution)/shard_map/pair_tiles/pallas_call | solution.py:140
  147.6 0.0 all-to-all-done.1.packed_ref
  147.6 0.0 copy-done.4
  147.6 7.7 %assemble.4.right_ref = bf16[1280,1280]{1,0:T(8,128)(2,1)S(1)} custom-call(s32[56]{0:T(128)S(1)} %copy-done.4, bf16[8,1,7,128,128]{4,3,2,1,0:T(8,128)(2,1)S(1)} %all-to-all-done.1.packed_ref), custom_call_target="tpu_custom_call" | custom-call | bytes 6553600 | tf_op jit(solution)/shard_map/assemble/pallas_call | solution.py:49
  155.3 0.0 copy-start.2
  155.3 1.6 copy-done.2
  156.9 22.9 %pair_tiles.4.rest_0_ = f32[4,8,3,7,32,128]{5,4,3,2,1,0:T(8,128)} custom-call(s32[56]{0:T(128)} %slot_ref.11, bf16[1280,1280]{1,0:T(8,128)(2,1)} %copy-done.1, bf16[1280,1280]{1,0:T(8,128)(2,1)} %copy-done.2, bf16[1,3,1200,1200]{3,2,1,0:T(8,128)(2,1)} %wr_ref.5, bf16[1,3,1200,1200]{3,2,1,0:T(8,128)(2,1)} %wr_ref.5, ...), custom_call_target="tpu_custom_call", output_to_operand_aliasing={{}: (5, {})} | custom-call | flops 8388608000 | bytes 26214400 | tf_op jit(solution)/shard_map/pair_tiles/pallas_call | solution.py:140
  179.8 23.0 %pair_tiles.5 = f32[4,8,3,7,32,128]{5,4,3,2,1,0:T(8,128)} custom-call(s32[56]{0:T(128)} %slot_ref.11, bf16[1280,1280]{1,0:T(8,128)(2,1)} %copy-done, bf16[1280,1280]{1,0:T(8,128)(2,1)} %copy-done.2, bf16[1,3,1200,1200]{3,2,1,0:T(8,128)(2,1)} %wr_ref.5, bf16[1,3,1200,1200]{3,2,1,0:T(8,128)(2,1)} %wr_ref.5, ...), custom_call_target="tpu_custom_call", output_to_operand_aliasing={{}: (5, {})} | custom-call | flops 8388608000 | bytes 26214400 | tf_op jit(solution)/shard_map/pair_tiles/pallas_call | solution.py:140
  202.9 0.0 reduce-scatter.2.cloned.1.call-update
  202.9 145.5 %reduce-scatter.2.cloned.1.call-done = f32[1,3,7,32,128]{4,3,2,1,0:T(8,128)} async-done(((f32[32,3,7,32,128]{4,3,2,1,0:T(8,128)}), f32[1,3,7,32,128]{4,3,2,1,0:T(8,128)}) %reduce-scatter.2.cloned.1.call-update) | async-done | bytes 344080 | tf_op jit(solution)/shard_map/reduce_scatter | solution.py:192
Async XLA Ops:
  10.9 89.2 %all-to-all-start = ((bf16[8,2,7,128,128]{4,3,2,1,0:T(8,128)(2,1)}), bf16[8,2,7,128,128]{4,3,2,1,0:T(8,128)(2,1)}, u32[]{:S(2)}, u32[]{:S(2)}) async-start(bf16[8,2,7,128,128]{4,3,2,1,0:T(8,128)(2,1)} %slice.6), calls=%async_computation | async-start | bytes 7340032 | tf_op jit(solution)/shard_map/all_to_all | solution.py:179
  17.2 86.5 %copy-start.3 = (s32[56]{0:T(128)S(1)}, s32[56]{0:T(128)}, u32[]{:S(2)}) copy-start(s32[56]{0:T(128)} %slot_ref.11) | copy-start | bytes 676
  100.1 47.5 %all-to-all-start.1 = ((bf16[8,1,7,128,128]{4,3,2,1,0:T(8,128)(2,1)}), bf16[8,1,7,128,128]{4,3,2,1,0:T(8,128)(2,1)S(1)}, u32[]{:S(2)}, u32[]{:S(2)}) async-start(bf16[8,1,7,128,128]{4,3,2,1,0:T(8,128)(2,1)} %slice.7), calls=%async_computation.1 | async-start | bytes 3670016 | tf_op jit(solution)/shard_map/all_to_all | solution.py:181
  103.7 244.7 %reduce-scatter.2.cloned.1.call-start = ((), (), s32[]{:S(2)}) async-start(), calls=%async_computation.3 | async-start | bytes 11354112 | tf_op jit(solution)/shard_map/reduce_scatter | solution.py:192
  112.4 1.7 copy-start.1
  122.7 1.8 copy-start
  124.5 23.0 %copy-start.4 = (s32[56]{0:T(128)S(1)}, s32[56]{0:T(128)}, u32[]{:S(2)}) copy-start(s32[56]{0:T(128)} %slot_ref.11) | copy-start | bytes 676
  155.3 1.7 copy-start.2
Sparse Core Ops, SparseCore 0:
  203.0 145.3 reduce-scatter.1
where the time goes:
time: 356 us; the launch traced here: 355 us
  waiting for transfers between devices  225 us (63%)
  Pallas kernels  94 us (26%)
  between operations  13.5 us (4%)
  local copies, waits for them, and re-layouts  12.4 us (3%)
  starting transfers between devices  9.99 us (3%)
    reduce_scatter x1, waiting for transfers between devices, local(): lax.psum_scatter(arranged, ('slab', 'blk'), scatter_dimension=0, tiled=True)  145 us
    all_to_all x1, waiting for transfers between devices, local(): lax.all_to_all(amplitudes[:, :last], 'blk', split_axis=0, concat_axis=0,...  79.8 us
    pallas_call x3, Pallas kernels, pair_tiles(): pl.pallas_call(functools.partial(pair_kernel, blocks, n_slab, n_blk), gri...  69 us
    pallas_call x3, Pallas kernels, assemble(): pl.pallas_call(functools.partial(assemble_kernel, v_width, blocks), grid=...  25 us
  transfers between devices with their start and end apart: 3, of which 2 were waited for; matrix products, arithmetic and copies ran while one was open for 1% of the time, Pallas kernels for 11%

commit v1 on v0

v1 whole, which is shorter than its diff:
```python
import functools

import jax
import jax.numpy as jnp
from jax import lax
from jax.experimental import pallas as pl
from jax.experimental.pallas import tpu as pltpu
from jax.sharding import PartitionSpec as P

MESH = pl.DeviceIdType.MESH


def flip(index, mask):
    out = index
    bit = 1
    while bit <= mask:
        if mask & bit:
            out = out + bit * (1 - 2 * ((index // bit) % 2))
        bit *= 2
    return out


def row_chunk(rows):
    return max(size for size in range(16, 257, 16) if rows % size == 0)


def cycle_kernel(
    dims,
    from_ref, tile_ref, amp_ref, int_ref, out_ref,
    packed0, packed1, packed2, full0, full1, full2, landing, weights, acc_a, acc_b,
    outgoing, mates, first_in, second_in, last_in,
    load_sem, local_sem, amp_send, amp_recv, mate_send, mate_recv,
    first_send, first_recv, second_send, second_recv, last_send, last_recv,
):
    n_slab, n_blk, blocks, v_width, slot_dev, tile_len = dims
    n_z = n_blk // 2
    half_z = n_z // 2
    padded = blocks * tile_len
    row_part = tile_len // n_slab
    n_slots = n_blk * slot_dev
    packed = (packed0, packed1, packed2)
    fulls = (full0, full1, full2)
    slab = lax.axis_index("slab")
    blk = lax.axis_index("blk")
    core = blk % 2
    z_at = blk // 2

    barrier = pltpu.get_barrier_semaphore()
    for mask in range(1, n_blk):
        pl.semaphore_signal(barrier, inc=1, device_id={"blk": flip(blk, mask)}, device_id_type=MESH)
    for mask in (1, 2):
        pl.semaphore_signal(barrier, inc=1, device_id={"slab": flip(slab, mask)}, device_id_type=MESH)
    pl.semaphore_wait(barrier, n_blk + 1)

    def amp_copy(which, mask):
        target = flip(blk, mask)
        return pltpu.make_async_remote_copy(
            src_ref=amp_ref.at[target, which],
            dst_ref=packed[which].at[blk],
            send_sem=amp_send.at[which, mask],
            recv_sem=amp_recv.at[which, mask],
            device_id={"blk": target},
            device_id_type=MESH,
        )

    def own_copy(which):
        return pltpu.make_async_copy(amp_ref.at[blk, which], packed[which].at[blk], local_sem.at[which])

    for which in range(3):
        for mask in reversed(range(1, n_blk)):
            amp_copy(which, mask).start()
        own_copy(which).start()

    chunk = landing.shape[1]
    n_chunk = v_width // chunk
    pad = padded - v_width

    def int_copy(number):
        which, at = divmod(number, n_chunk)
        return pltpu.make_async_copy(
            int_ref.at[0, which, pl.ds(at * chunk, chunk)], landing.at[number % 2], load_sem.at[number % 2]
        )

    int_copy(0).start()
    for number in range(3 * n_chunk):
        which, at = divmod(number, n_chunk)
        if number + 1 < 3 * n_chunk:
            int_copy(number + 1).start()
        int_copy(number).wait()
        weights[which, pl.ds(at * chunk, chunk), pl.ds(0, v_width)] = landing[number % 2]
    if pad:
        for which in range(3):
            weights[which, :, pl.ds(v_width, pad)] = jnp.zeros((padded, pad), weights.dtype)
            weights[which, pl.ds(v_width, pad), :] = jnp.zeros((pad, padded), weights.dtype)

    row_ids = lax.broadcasted_iota(jnp.int32, (tile_len, tile_len), 0)
    col_ids = lax.broadcasted_iota(jnp.int32, (tile_len, tile_len), 1)

    def put_tile(which, x, y):
        at = x * blocks + y
        rows = pl.ds(pl.multiple_of(x * tile_len, tile_len), tile_len)
        cols = pl.ds(pl.multiple_of(y * tile_len, tile_len), tile_len)
        keep = jnp.logical_and(row_ids + x * tile_len < col_ids + y * tile_len, col_ids + y * tile_len < v_width)
        raw = packed[which][from_ref[0, at], from_ref[1, at]]
        tile = jnp.where(keep, raw.astype(jnp.float32), 0.0)
        mirror = tile.T
        same = jnp.where(x == y, 1.0, 0.0)
        fulls[which][rows, cols] = (tile - same * mirror).astype(raw.dtype)
        fulls[which][cols, rows] = (same * tile - mirror).astype(raw.dtype)

    def build(which):
        for mask in range(1, n_blk):
            amp_copy(which, mask).wait_recv()
        own_copy(which).wait()
        if blocks % 2:
            for x in range(blocks):
                for y in range(x, blocks):
                    put_tile(which, x, y)
            return

        def fold(i, carry):
            for j in range(blocks + 1):
                upper = j < blocks - i
                x = jnp.where(upper, i, blocks - 1 - i)
                y = jnp.where(upper, i + j, j - 1)
                put_tile(which, x, y)
            return carry

        lax.fori_loop(0, blocks // 2, fold, 0)

    width = 2 * tile_len if padded % (2 * tile_len) == 0 else tile_len

    per_step = width // tile_len

    def product(left, right, cols):
        return jnp.dot(fulls[left][...], weights[right, :, cols], preferred_element_type=jnp.float32)

    def by_columns(acc, fresh, terms):
        def step(number, carry):
            cols = pl.ds(pl.multiple_of(number * width, width), width)
            total = None
            for sign, left, right in terms:
                term = product(left, right, cols)
                total = (term if sign > 0 else -term) if total is None else total + term if sign > 0 else total - term
            for x in range(blocks):
                for part in range(per_step):
                    y = number * per_step + part
                    tile = total[x * tile_len : (x + 1) * tile_len, part * tile_len : (part + 1) * tile_len]
                    acc[x, y] = tile if fresh else acc[x, y] + tile
            return carry

        lax.fori_loop(0, padded // width, step, 0)

    def pack(acc):
        def owner_tiles(owner, carry):
            for place in range(slot_dev):
                slot = owner * slot_dev + place
                first, second, used = tile_ref[0, slot], tile_ref[1, slot], tile_ref[2, slot]
                tile = (acc[first, second] - acc[second, first].T) * used.astype(jnp.float32)
                for part in range(n_slab):
                    outgoing[owner % 2, part, owner // 2, place] = tile[part * row_part : (part + 1) * row_part]
            return carry

        lax.fori_loop(0, n_blk, owner_tiles, 0)

    def mate_copy(pair, mask):
        part = flip(slab, mask)
        return pltpu.make_async_remote_copy(
            src_ref=outgoing.at[1 - core, part],
            dst_ref=mates.at[pair, part],
            send_sem=mate_send.at[pair, mask],
            recv_sem=mate_recv.at[pair, mask],
            device_id={"blk": flip(blk, 1)},
            device_id_type=MESH,
        )

    halves = (pl.ds(0, half_z), pl.ds(half_z, n_z - half_z))

    def first_copy(pair, half, far):
        mine, other = (1, 2) if half == 0 else (2, 1)
        part = flip(slab, 3 if far else mine)
        return pltpu.make_async_remote_copy(
            src_ref=mates.at[pair, part, halves[half]],
            dst_ref=first_in.at[pair, half, far],
            send_sem=first_send.at[pair, half, far],
            recv_sem=first_recv.at[pair, half, far],
            device_id={"slab": flip(slab, mine)},
            device_id_type=MESH,
        )

    def second_copy(pair, half):
        other = 2 if half == 0 else 1
        return pltpu.make_async_remote_copy(
            src_ref=mates.at[pair, flip(slab, other), halves[half]],
            dst_ref=second_in.at[pair, half],
            send_sem=second_send.at[pair, half],
            recv_sem=second_recv.at[pair, half],
            device_id={"slab": flip(slab, other)},
            device_id_type=MESH,
        )

    def last_copy(pair, mask):
        target = flip(z_at, mask)
        return pltpu.make_async_remote_copy(
            src_ref=mates.at[pair, slab, target],
            dst_ref=last_in.at[pair, mask],
            send_sem=last_send.at[pair, mask],
            recv_sem=last_recv.at[pair, mask],
            device_id={"blk": target * 2 + core},
            device_id_type=MESH,
        )

    def mates_start(pair):
        for mask in (3, 1, 2, 0):
            mate_copy(pair, mask).start()

    def mates_finish(pair):
        for mask in (3, 1, 2, 0):
            mate_copy(pair, mask).wait_recv()
            part = flip(slab, mask)
            mates[pair, part] = mates[pair, part] + outgoing[core, part]
            if mask == 3:
                first_copy(pair, 0, 1).start()
                first_copy(pair, 1, 1).start()
            if mask == 1:
                first_copy(pair, 0, 0).start()
            if mask == 2:
                first_copy(pair, 1, 0).start()
        for mask in (3, 1, 2, 0):
            mate_copy(pair, mask).wait_send()

    def first_finish(pair):
        for half in (0, 1):
            part = flip(slab, 2 if half == 0 else 1)
            first_copy(pair, half, 1).wait_recv()
            mates[pair, part, halves[half]] = mates[pair, part, halves[half]] + first_in[pair, half, 1]
            second_copy(pair, half).start()

    def second_finish(pair):
        for half in (0, 1):
            first_copy(pair, half, 0).wait_recv()
            second_copy(pair, half).wait_recv()
            mates[pair, slab, halves[half]] = (
                mates[pair, slab, halves[half]] + first_in[pair, half, 0] + second_in[pair, half]
            )

    def last_start(pair):
        for mask in reversed(range(1, n_z)):
            last_copy(pair, mask).start()

    def last_finish(pair):
        total = mates[pair, slab, z_at]
        for mask in range(1, n_z):
            last_copy(pair, mask).wait_recv()
            total = total + last_in[pair, mask]
        out_ref[pair] = total

    pair01, pair02, pair12 = 0, 1, 2
    build(0)
    build(1)

    by_columns(acc_a, True, ((1, 0, 1), (-1, 1, 0)))
    pack(acc_a)
    mates_start(pair01)

    by_columns(acc_b, True, ((1, 0, 2),))
    mates_finish(pair01)

    by_columns(acc_a, True, ((1, 1, 2),))
    first_finish(pair01)
    second_finish(pair01)

    build(2)
    last_start(pair01)

    by_columns(acc_b, False, ((-1, 2, 0),))
    pack(acc_b)
    mates_start(pair02)

    by_columns(acc_a, False, ((-1, 2, 1),))
    mates_finish(pair02)
    pack(acc_a)
    mates_start(pair12)
    mates_finish(pair12)
    first_finish(pair02)
    second_finish(pair02)
    last_start(pair02)
    first_finish(pair12)
    last_finish(pair01)
    second_finish(pair12)
    last_start(pair12)
    last_finish(pair02)
    last_finish(pair12)

    for which in range(3):
        for mask in range(1, n_blk):
            amp_copy(which, mask).wait_send()
    for pair in (pair01, pair02, pair12):
        for half in (0, 1):
            for far in (0, 1):
                first_copy(pair, half, far).wait_send()
            second_copy(pair, half).wait_send()
        for mask in range(1, n_z):
            last_copy(pair, mask).wait_send()


def local(amplitudes, integrals, slot_tile):
    n_slab = lax.axis_size("slab")
    n_blk = lax.axis_size("blk")
    n_out, slot_dev, tile_len = amplitudes.shape[1:4]
    v_width = integrals.shape[-1]
    blocks = (v_width + tile_len - 1) // tile_len
    padded = blocks * tile_len
    row_part = tile_len // n_slab
    n_z = n_blk // 2
    half_z = n_z // 2
    assert n_slab == 4 and n_out == 3 and n_blk & (n_blk - 1) == 0 and n_blk >= 4
    bf16, f32 = amplitudes.dtype, jnp.float32
    piece = (slot_dev, row_part, tile_len)
    dma = pltpu.SemaphoreType.DMA
    n_slots = slot_tile.shape[0]
    slot_ids = jnp.arange(n_slots, dtype=jnp.int32)
    tile_ids = jnp.arange(blocks * blocks, dtype=jnp.int32)
    slot_of = jnp.sum(jnp.where(slot_tile[None] == tile_ids[:, None], slot_ids[None], 0), axis=1)
    come_from = jnp.stack([slot_of // slot_dev, slot_of % slot_dev])
    used = slot_tile >= 0
    safe = jnp.maximum(slot_tile, 0)
    tile_at = jnp.stack([safe // blocks, safe % blocks, used.astype(jnp.int32)])
    dims = (n_slab, n_blk, blocks, v_width, slot_dev, tile_len)
    return pl.pallas_call(
        functools.partial(cycle_kernel, dims),
        out_shape=jax.ShapeDtypeStruct((n_out,) + piece, f32),
        in_specs=[
            pl.BlockSpec(memory_space=pltpu.SMEM),
            pl.BlockSpec(memory_space=pltpu.SMEM),
            pl.BlockSpec(memory_space=pl.ANY),
            pl.BlockSpec(memory_space=pl.ANY),
        ],
        out_specs=pl.BlockSpec(memory_space=pltpu.VMEM),
        scratch_shapes=[pltpu.VMEM((n_blk, slot_dev, tile_len, tile_len), bf16)] * 3
        + [pltpu.VMEM((padded, padded), bf16)] * 3
        + [
            pltpu.VMEM((2, row_chunk(v_width), v_width), bf16),
            pltpu.VMEM((3, padded, padded), bf16),
            pltpu.VMEM((blocks, blocks, tile_len, tile_len), f32),
            pltpu.VMEM((blocks, blocks, tile_len, tile_len), f32),
            pltpu.VMEM((2, n_slab, n_z) + piece, f32),
            pltpu.VMEM((3, n_slab, n_z) + piece, f32),
            pltpu.VMEM((3, 2, 2, half_z) + piece, f32),
            pltpu.VMEM((3, 2, half_z) + piece, f32),
            pltpu.VMEM((3, n_z) + piece, f32),
            dma((2,)),
            dma((3,)),
            dma((3, n_blk)),
            dma((3, n_blk)),
            dma((3, 4)),
            dma((3, 4)),
            dma((3, 2, 2)),
            dma((3, 2, 2)),
            dma((3, 2)),
            dma((3, 2)),
            dma((3, n_z)),
            dma((3, n_z)),
        ],
        compiler_params=pltpu.CompilerParams(
            collective_id=0, has_side_effects=True, vmem_limit_bytes=67043328
        ),
        name="cycle",
    )(come_from, tile_at, amplitudes, integrals)


def solution(mesh):
    return jax.shard_map(
        local,
        mesh=mesh,
        in_specs=(P("slab", None, "blk", None, None), P(("slab", "blk"), None, None, None), P()),
        out_specs=P(None, "blk", "slab", None),
        check_vma=False,
    )
```

time: 356 us -> 202 us (0.57)
  waiting for transfers between devices: 225 us -> 0 us
  Pallas kernels: 94 us -> 197 us
  between operations: 13.5 us -> 0.01 us
  local copies, waits for them, and re-layouts: 12.4 us -> 1.73 us
  starting transfers between devices: 9.99 us -> 0 us
    reduce_scatter x1 -> x0, waiting for transfers between devices: 145 us -> none  [local(): lax.psum_scatter(arranged, ('slab', 'blk'), scatter_dimension=0, tiled=True)]
    pallas_call x6 -> x1, Pallas kernels: 94 us -> 197 us  [local(): pl.pallas_call(functools.partial(cycle_kernel, dims), out_shape=jax.Shape...]
    all_to_all x2 -> x0, waiting for transfers between devices: 79.8 us -> none  [the longest x1 79.8 us: local(): lax.all_to_all(amplitudes[:, :last], 'blk', split_axis=0, concat_axis=0,...]
    all_to_all x2 -> x0, starting transfers between devices: 9.95 us -> none  [the longest x1 6.35 us: local(): lax.all_to_all(amplitudes[:, :last], 'blk', split_axis=0, concat_axis=0,...]
    slice x2 -> x0, local copies, waits for them, and re-layouts: 7.35 us -> none  [the longest x1 4.36 us: local(): amplitudes[:, :last]]
  transfers between devices with their start and end apart: 3 -> 0, of which waited for: 2 -> 0; matrix products, arithmetic and copies ran while one was open for 1% -> 0% of each run, Pallas kernels for 11% -> 0%
where the time goes in v1:
time: 202 us
  Pallas kernels  197 us (98%)
  other arithmetic  3.28 us (2%)
    pallas_call x1, Pallas kernels, local(): pl.pallas_call(functools.partial(cycle_kernel, dims), out_shape=jax.Shape...  197 us

profile of v1, /device:TPU:0, one launch (start us, length us, event | category | flops | bytes accessed | tf_op | source)
XLA Modules:
  0.0 202.1 jit_solution(640037226968644238)
XLA Ops:
  0.0 0.7 select_reduce_fusion
  0.7 0.7 fusion.2
  1.4 0.6 pad_add_fusion.1.from_ref
  2.0 0.7 fusion.3
  2.7 0.6 pad_add_fusion.tile_ref
  3.3 197.1 %cycle.1 = f32[3,7,32,128]{3,2,1,0:T(8,128)} custom-call(s32[2,100]{1,0:T(2,128)} %pad_add_fusion.1.from_ref, s32[3,56]{1,0:T(4,128)} %pad_add_fusion.tile_ref, bf16[8,3,7,128,128]{4,3,2,1,0:T(8,128)(2,1)} %amp_ref.1, bf16[1,3,1200,1200]{3,2,1,0:T(8,128)(2,1)} %int_ref.1), custom_call_target="tpu_custom_call" | custom-call | tf_op jit(solution)/shard_map/cycle/pallas_call | solution.py:330
  200.4 1.7 copy.5
  (1 shorter events, 0.0 us)

commit v2 on v1

--- a/solution.py
+++ b/solution.py
@@ -26,7 +26,7 @@
 
 def cycle_kernel(
     dims,
-    from_ref, tile_ref, amp_ref, int_ref, out_ref,
+    of_ref, slot_ref, amp_ref, int_ref, out_ref,
     packed0, packed1, packed2, full0, full1, full2, landing, weights, acc_a, acc_b,
     outgoing, mates, first_in, second_in, last_in,
     load_sem, local_sem, amp_send, amp_recv, mate_send, mate_recv,
@@ -66,9 +66,11 @@
     def own_copy(which):
         return pltpu.make_async_copy(amp_ref.at[blk, which], packed[which].at[blk], local_sem.at[which])
 
+    order = tuple(reversed(range(1, n_blk)))
     for which in range(3):
-        for mask in reversed(range(1, n_blk)):
-            amp_copy(which, mask).start()
+        if which < 2:
+            for mask in order:
+                amp_copy(which, mask).start()
         own_copy(which).start()
 
     chunk = landing.shape[1]
@@ -93,6 +95,11 @@
             weights[which, :, pl.ds(v_width, pad)] = jnp.zeros((padded, pad), weights.dtype)
             weights[which, pl.ds(v_width, pad), :] = jnp.zeros((pad, padded), weights.dtype)
 
+    gate = n_blk // 2
+    amp_copy(1, gate).wait_recv()
+    for mask in order:
+        amp_copy(2, mask).start()
+
     row_ids = lax.broadcasted_iota(jnp.int32, (tile_len, tile_len), 0)
     col_ids = lax.broadcasted_iota(jnp.int32, (tile_len, tile_len), 1)
 
@@ -101,7 +108,7 @@
         rows = pl.ds(pl.multiple_of(x * tile_len, tile_len), tile_len)
         cols = pl.ds(pl.multiple_of(y * tile_len, tile_len), tile_len)
         keep = jnp.logical_and(row_ids + x * tile_len < col_ids + y * tile_len, col_ids + y * tile_len < v_width)
-        raw = packed[which][from_ref[0, at], from_ref[1, at]]
+        raw = packed[which][lax.div(of_ref[at], slot_dev), lax.rem(of_ref[at], slot_dev)]
         tile = jnp.where(keep, raw.astype(jnp.float32), 0.0)
         mirror = tile.T
         same = jnp.where(x == y, 1.0, 0.0)
@@ -110,7 +117,8 @@
 
     def build(which):
         for mask in range(1, n_blk):
-            amp_copy(which, mask).wait_recv()
+            if (which, mask) != (1, gate):
+                amp_copy(which, mask).wait_recv()
         own_copy(which).wait()
         if blocks % 2:
             for x in range(blocks):
@@ -155,7 +163,9 @@
         def owner_tiles(owner, carry):
             for place in range(slot_dev):
                 slot = owner * slot_dev + place
-                first, second, used = tile_ref[0, slot], tile_ref[1, slot], tile_ref[2, slot]
+                tile_id = jnp.maximum(slot_ref[slot], 0)
+                used = jnp.minimum(slot_ref[slot], 0) + 1
+                first, second = lax.div(tile_id, blocks), lax.rem(tile_id, blocks)
                 tile = (acc[first, second] - acc[second, first].T) * used.astype(jnp.float32)
                 for part in range(n_slab):
                     outgoing[owner % 2, part, owner // 2, place] = tile[part * row_part : (part + 1) * row_part]
@@ -281,8 +291,8 @@
     mates_finish(pair02)
     pack(acc_a)
     mates_start(pair12)
+    first_finish(pair02)
     mates_finish(pair12)
-    first_finish(pair02)
     second_finish(pair02)
     last_start(pair02)
     first_finish(pair12)
@@ -322,10 +332,6 @@
     slot_ids = jnp.arange(n_slots, dtype=jnp.int32)
     tile_ids = jnp.arange(blocks * blocks, dtype=jnp.int32)
     slot_of = jnp.sum(jnp.where(slot_tile[None] == tile_ids[:, None], slot_ids[None], 0), axis=1)
-    come_from = jnp.stack([slot_of // slot_dev, slot_of % slot_dev])
-    used = slot_tile >= 0
-    safe = jnp.maximum(slot_tile, 0)
-    tile_at = jnp.stack([safe // blocks, safe % blocks, used.astype(jnp.int32)])
     dims = (n_slab, n_blk, blocks, v_width, slot_dev, tile_len)
     return pl.pallas_call(
         functools.partial(cycle_kernel, dims),
@@ -366,7 +372,7 @@
             collective_id=0, has_side_effects=True, vmem_limit_bytes=67043328
         ),
         name="cycle",
-    )(come_from, tile_at, amplitudes, integrals)
+    )(slot_of, slot_tile, amplitudes, integrals)
 
 
 def solution(mesh):

time: 202 us -> 183 us (0.906)
  Pallas kernels: 197 us -> 179 us
    pallas_call x1, Pallas kernels: 197 us -> 179 us  [local(): pl.pallas_call(functools.partial(cycle_kernel, dims), out_shape=jax.Shape...]
    another operation x4 -> x0, other arithmetic: 2.52 us -> none  [the longest x3 1.92 us: local(): tile_at = jnp.stack([safe // blocks, safe % blocks, used.astype(jnp.int32)])]
where the time goes in v2:
time: 183 us; the launch traced here: 182 us
  Pallas kernels  179 us (98%)
    pallas_call x1, Pallas kernels, local(): pl.pallas_call(functools.partial(cycle_kernel, dims), out_shape=jax.Shape...  179 us

profile of v2, /device:TPU:0, one launch (start us, length us, event | category | flops | bytes accessed | tf_op | source)
XLA Modules:
  0.0 182.3 jit_solution(7228017690449334297)
XLA Ops:
  0.0 1.3 select_reduce_fusion.of_ref
  1.3 179.3 %cycle.1 = f32[3,7,32,128]{3,2,1,0:T(8,128)} custom-call(s32[100]{0:T(128)} %select_reduce_fusion.of_ref, s32[56]{0:T(128)} %slot_ref.1, bf16[8,3,7,128,128]{4,3,2,1,0:T(8,128)(2,1)} %amp_ref.1, bf16[1,3,1200,1200]{3,2,1,0:T(8,128)(2,1)} %int_ref.1), custom_call_target="tpu_custom_call" | custom-call | tf_op jit(solution)/shard_map/cycle/pallas_call | solution.py:336
  180.6 1.7 copy.5

commit v3 on v2

--- a/solution.py
+++ b/solution.py
@@ -8,6 +8,8 @@
 from jax.sharding import PartitionSpec as P
 
 MESH = pl.DeviceIdType.MESH
+PARTS = (3, 1, 2, 0)
+EARLY = 2
 
 
 def flip(index, mask):
@@ -20,6 +22,10 @@
     return out
 
 
+def plain_places(slot_dev):
+    return max(1, slot_dev * 5 // 7), max(1, slot_dev * 5 // 7)
+
+
 def row_chunk(rows):
     return max(size for size in range(16, 257, 16) if rows % size == 0)
 
@@ -28,14 +34,22 @@
     dims,
     of_ref, slot_ref, amp_ref, int_ref, out_ref,
     packed0, packed1, packed2, full0, full1, full2, landing, weights, acc_a, acc_b,
-    outgoing, mates, first_in, second_in, last_in,
-    load_sem, local_sem, amp_send, amp_recv, mate_send, mate_recv,
+    outgoing, mates, low_in, first_in, second_in, last_in,
+    load_sem, local_sem, amp_send, amp_recv, mate_send, mate_recv, low_send, low_recv,
     first_send, first_recv, second_send, second_recv, last_send, last_recv,
 ):
     n_slab, n_blk, blocks, v_width, slot_dev, tile_len = dims
     n_z = n_blk // 2
-    half_z = n_z // 2
     padded = blocks * tile_len
+    cut = plain_places(slot_dev)
+    jobs = (
+        (0, pl.ds(0, slot_dev), False),
+        (1, pl.ds(0, cut[0]), False),
+        (1, pl.ds(cut[0], slot_dev - cut[0]), True),
+        (2, pl.ds(0, cut[1]), False),
+        (2, pl.ds(cut[1], slot_dev - cut[1]), True),
+    )
+    whole01, plain02, low02, plain12, low12 = range(5)
     row_part = tile_len // n_slab
     n_slots = n_blk * slot_dev
     packed = (packed0, packed1, packed2)
@@ -115,11 +129,13 @@
         fulls[which][rows, cols] = (tile - same * mirror).astype(raw.dtype)
         fulls[which][cols, rows] = (same * tile - mirror).astype(raw.dtype)
 
-    def build(which):
+    def arrive(which):
         for mask in range(1, n_blk):
             if (which, mask) != (1, gate):
                 amp_copy(which, mask).wait_recv()
         own_copy(which).wait()
+
+    def build(which):
         if blocks % 2:
             for x in range(blocks):
                 for y in range(x, blocks):
@@ -143,7 +159,7 @@
     def product(left, right, cols):
         return jnp.dot(fulls[left][...], weights[right, :, cols], preferred_element_type=jnp.float32)
 
-    def by_columns(acc, fresh, terms):
+    def by_columns(acc, fresh, terms, start=0, stop=padded // width):
         def step(number, carry):
             cols = pl.ds(pl.multiple_of(number * width, width), width)
             total = None
@@ -157,161 +173,220 @@
                     acc[x, y] = tile if fresh else acc[x, y] + tile
             return carry
 
-        lax.fori_loop(0, padded // width, step, 0)
-
-    def pack(acc):
-        def owner_tiles(owner, carry):
-            for place in range(slot_dev):
-                slot = owner * slot_dev + place
-                tile_id = jnp.maximum(slot_ref[slot], 0)
-                used = jnp.minimum(slot_ref[slot], 0) + 1
-                first, second = lax.div(tile_id, blocks), lax.rem(tile_id, blocks)
-                tile = (acc[first, second] - acc[second, first].T) * used.astype(jnp.float32)
-                for part in range(n_slab):
-                    outgoing[owner % 2, part, owner // 2, place] = tile[part * row_part : (part + 1) * row_part]
-            return carry
-
-        lax.fori_loop(0, n_blk, owner_tiles, 0)
+        lax.fori_loop(start, stop, step, 0)
+
+    def pack(acc, pair):
+        def tiles_of(core_at):
+            def owner_tiles(z, carry):
+                for place in range(slot_dev):
+                    slot = (z * 2 + core_at) * slot_dev + place
+                    tile_id = jnp.maximum(slot_ref[slot], 0)
+                    used = jnp.minimum(slot_ref[slot], 0) + 1
+                    first, second = lax.div(tile_id, blocks), lax.rem(tile_id, blocks)
+                    tile = (acc[first, second] - acc[second, first].T) * used.astype(jnp.float32)
+                    for part in range(n_slab):
+                        rows = tile[part * row_part : (part + 1) * row_part]
+                        outgoing[core_at, part // 2, part % 2, z // 2, z % 2, place] = rows
+                return carry
+
+            lax.fori_loop(0, n_z, owner_tiles, 0)
+
+        tiles_of(1 - core)
+        for mask in PARTS:
+            mate_copy(pair, mask).start()
+        tiles_of(core)
+
+    s_y, s_x = slab // 2, slab % 2
+    z_hi, z_lo = z_at // 2, z_at % 2
+    n_hi = n_z // 2
+    halves = (pl.ds(0, n_hi // 2), pl.ds(n_hi // 2, n_hi - n_hi // 2))
+
+    def part_of(mask):
+        return (1 - s_y if mask & 2 else s_y), (1 - s_x if mask & 1 else s_x)
 
     def mate_copy(pair, mask):
-        part = flip(slab, mask)
-        return pltpu.make_async_remote_copy(
-            src_ref=outgoing.at[1 - core, part],
-            dst_ref=mates.at[pair, part],
+        p_y, p_x = part_of(mask)
+        return pltpu.make_async_remote_copy(
+            src_ref=outgoing.at[1 - core, p_y, p_x],
+            dst_ref=mates.at[pair, p_y, p_x],
             send_sem=mate_send.at[pair, mask],
             recv_sem=mate_recv.at[pair, mask],
             device_id={"blk": flip(blk, 1)},
             device_id_type=MESH,
         )
 
-    halves = (pl.ds(0, half_z), pl.ds(half_z, n_z - half_z))
-
-    def first_copy(pair, half, far):
-        mine, other = (1, 2) if half == 0 else (2, 1)
-        part = flip(slab, 3 if far else mine)
-        return pltpu.make_async_remote_copy(
-            src_ref=mates.at[pair, part, halves[half]],
-            dst_ref=first_in.at[pair, half, far],
-            send_sem=first_send.at[pair, half, far],
-            recv_sem=first_recv.at[pair, half, far],
+    def low_copy(job, mask):
+        pair, places, _ = jobs[job]
+        p_y, p_x = part_of(mask)
+        return pltpu.make_async_remote_copy(
+            src_ref=mates.at[pair, p_y, p_x, :, 1 - z_lo, places],
+            dst_ref=low_in.at[pair, p_y, p_x, :, places],
+            send_sem=low_send.at[job, mask],
+            recv_sem=low_recv.at[job, mask],
+            device_id={"blk": flip(blk, 2)},
+            device_id_type=MESH,
+        )
+
+    def z_range(job):
+        return z_lo if jobs[job][2] else slice(None)
+
+    def first_copy(job, half, far):
+        pair, places, _ = jobs[job]
+        mine = 1 if half == 0 else 2
+        p_y, p_x = part_of(3 if far else mine)
+        return pltpu.make_async_remote_copy(
+            src_ref=mates.at[pair, p_y, p_x, halves[half], z_range(job), places],
+            dst_ref=first_in.at[pair, half, far, :, z_range(job), places],
+            send_sem=first_send.at[job, half, far],
+            recv_sem=first_recv.at[job, half, far],
             device_id={"slab": flip(slab, mine)},
             device_id_type=MESH,
         )
 
-    def second_copy(pair, half):
+    def second_copy(job, half):
+        pair, places, _ = jobs[job]
         other = 2 if half == 0 else 1
-        return pltpu.make_async_remote_copy(
-            src_ref=mates.at[pair, flip(slab, other), halves[half]],
-            dst_ref=second_in.at[pair, half],
-            send_sem=second_send.at[pair, half],
-            recv_sem=second_recv.at[pair, half],
+        p_y, p_x = part_of(other)
+        return pltpu.make_async_remote_copy(
+            src_ref=mates.at[pair, p_y, p_x, halves[half], z_range(job), places],
+            dst_ref=second_in.at[pair, half, :, z_range(job), places],
+            send_sem=second_send.at[job, half],
+            recv_sem=second_recv.at[job, half],
             device_id={"slab": flip(slab, other)},
             device_id_type=MESH,
         )
 
-    def last_copy(pair, mask):
+    def last_masks(job):
+        return [mask for mask in reversed(range(1, n_z)) if not (jobs[job][2] and mask % 2)]
+
+    def last_copy(job, mask):
+        pair, places, _ = jobs[job]
         target = flip(z_at, mask)
         return pltpu.make_async_remote_copy(
-            src_ref=mates.at[pair, slab, target],
-            dst_ref=last_in.at[pair, mask],
-            send_sem=last_send.at[pair, mask],
-            recv_sem=last_recv.at[pair, mask],
+            src_ref=mates.at[pair, s_y, s_x, target // 2, target % 2, places],
+            dst_ref=last_in.at[pair, mask, places],
+            send_sem=last_send.at[job, mask],
+            recv_sem=last_recv.at[job, mask],
             device_id={"blk": target * 2 + core},
             device_id_type=MESH,
         )
 
-    def mates_start(pair):
-        for mask in (3, 1, 2, 0):
-            mate_copy(pair, mask).start()
+    def first_start(job, mask):
+        if mask == 3:
+            first_copy(job, 0, 1).start()
+            first_copy(job, 1, 1).start()
+        elif mask:
+            first_copy(job, mask - 1, 0).start()
 
     def mates_finish(pair):
-        for mask in (3, 1, 2, 0):
+        for mask in PARTS:
             mate_copy(pair, mask).wait_recv()
-            part = flip(slab, mask)
-            mates[pair, part] = mates[pair, part] + outgoing[core, part]
-            if mask == 3:
-                first_copy(pair, 0, 1).start()
-                first_copy(pair, 1, 1).start()
-            if mask == 1:
-                first_copy(pair, 0, 0).start()
-            if mask == 2:
-                first_copy(pair, 1, 0).start()
-        for mask in (3, 1, 2, 0):
+            p_y, p_x = part_of(mask)
+            mates[pair, p_y, p_x] = mates[pair, p_y, p_x] + outgoing[core, p_y, p_x]
+            for job, (owner, _, low) in enumerate(jobs):
+                if owner == pair and low:
+                    low_copy(job, mask).start()
+                elif owner == pair:
+                    first_start(job, mask)
+        for mask in PARTS:
             mate_copy(pair, mask).wait_send()
 
-    def first_finish(pair):
+    def low_finish(job):
+        pair, places, _ = jobs[job]
+        for mask in PARTS:
+            low_copy(job, mask).wait_recv()
+            p_y, p_x = part_of(mask)
+            mates[pair, p_y, p_x, :, z_lo, places] = (
+                mates[pair, p_y, p_x, :, z_lo, places] + low_in[pair, p_y, p_x, :, places]
+            )
+            first_start(job, mask)
+
+    def first_finish(job):
+        pair, places, _ = jobs[job]
         for half in (0, 1):
-            part = flip(slab, 2 if half == 0 else 1)
-            first_copy(pair, half, 1).wait_recv()
-            mates[pair, part, halves[half]] = mates[pair, part, halves[half]] + first_in[pair, half, 1]
-            second_copy(pair, half).start()
-
-    def second_finish(pair):
+            at = (pair, *part_of(2 if half == 0 else 1), halves[half], z_range(job), places)
+            first_copy(job, half, 1).wait_recv()
+            mates[at] = mates[at] + first_in[pair, half, 1, :, z_range(job), places]
+            second_copy(job, half).start()
+
+    def second_finish(job):
+        pair, places, _ = jobs[job]
         for half in (0, 1):
-            first_copy(pair, half, 0).wait_recv()
-            second_copy(pair, half).wait_recv()
-            mates[pair, slab, halves[half]] = (
-                mates[pair, slab, halves[half]] + first_in[pair, half, 0] + second_in[pair, half]
+            at = (pair, s_y, s_x, halves[half], z_range(job), places)
+            first_copy(job, half, 0).wait_recv()
+            second_copy(job, half).wait_recv()
+            mates[at] = (
+                mates[at]
+                + first_in[pair, half, 0, :, z_range(job), places]
+                + second_in[pair, half, :, z_range(job), places]
             )
 
-    def last_start(pair):
-        for mask in reversed(range(1, n_z)):
-            last_copy(pair, mask).start()
-
-    def last_finish(pair):
-        total = mates[pair, slab, z_at]
-        for mask in range(1, n_z):
-            last_copy(pair, mask).wait_recv()
-            total = total + last_in[pair, mask]
-        out_ref[pair] = total
+    def last_start(job):
+        for mask in last_masks(job):
+            last_copy(job, mask).start()
+
+    def last_finish(job):
+        pair, places, _ = jobs[job]
+        total = mates[pair, s_y, s_x, z_hi, z_lo, places]
+        for mask in last_masks(job):
+            last_copy(job, mask).wait_recv()
+            total = total + last_in[pair, mask, places]
+        out_ref[pair, places] = total
 
     pair01, pair02, pair12 = 0, 1, 2
+    arrive(0)
     build(0)
+    arrive(1)
     build(1)
-
     by_columns(acc_a, True, ((1, 0, 1), (-1, 1, 0)))
-    pack(acc_a)
-    mates_start(pair01)
-
+    pack(acc_a, pair01)
     by_columns(acc_b, True, ((1, 0, 2),))
     mates_finish(pair01)
-
     by_columns(acc_a, True, ((1, 1, 2),))
-    first_finish(pair01)
-    second_finish(pair01)
-
+    first_finish(whole01)
+    second_finish(whole01)
+
+    arrive(2)
+    last_start(whole01)
     build(2)
-    last_start(pair01)
-
     by_columns(acc_b, False, ((-1, 2, 0),))
-    pack(acc_b)
-    mates_start(pair02)
-
-    by_columns(acc_a, False, ((-1, 2, 1),))
+    pack(acc_b, pair02)
+    by_columns(acc_a, False, ((-1, 2, 1),), 0, EARLY)
     mates_finish(pair02)
-    pack(acc_a)
-    mates_start(pair12)
-    first_finish(pair02)
+    by_columns(acc_a, False, ((-1, 2, 1),), EARLY)
+    first_finish(plain02)
+    pack(acc_a, pair12)
+    low_finish(low02)
     mates_finish(pair12)
-    second_finish(pair02)
-    last_start(pair02)
-    first_finish(pair12)
-    last_finish(pair01)
-    second_finish(pair12)
-    last_start(pair12)
-    last_finish(pair02)
-    last_finish(pair12)
-
-    for which in range(3):
-        for mask in range(1, n_blk):
-            amp_copy(which, mask).wait_send()
-    for pair in (pair01, pair02, pair12):
+    second_finish(plain02)
+    last_start(plain02)
+    first_finish(low02)
+    first_finish(plain12)
+    second_finish(low02)
+    last_start(low02)
+    low_finish(low12)
+    first_finish(low12)
+    second_finish(plain12)
+    last_start(plain12)
+    second_finish(low12)
+    last_start(low12)
+    for job in range(len(jobs)):
+        last_finish(job)
+
+    for mask in order:
+        amp_copy(0, mask).wait_send()
+        amp_copy(1, mask).wait_send()
+        amp_copy(2, mask).wait_send()
+    for job, (_, _, low) in enumerate(jobs):
+        for mask in PARTS:
+            if low:
+                low_copy(job, mask).wait_send()
         for half in (0, 1):
             for far in (0, 1):
-                first_copy(pair, half, far).wait_send()
-            second_copy(pair, half).wait_send()
-        for mask in range(1, n_z):
-            last_copy(pair, mask).wait_send()
+                first_copy(job, half, far).wait_send()
+            second_copy(job, half).wait_send()
+        for mask in last_masks(job):
+            last_copy(job, mask).wait_send()
 
 
 def local(amplitudes, integrals, slot_tile):
@@ -323,8 +398,9 @@
     padded = blocks * tile_len
     row_part = tile_len // n_slab
     n_z = n_blk // 2
-    half_z = n_z // 2
-    assert n_slab == 4 and n_out == 3 and n_blk & (n_blk - 1) == 0 and n_blk >= 4
+    half_hi = n_z // 4
+    n_jobs = 5
+    assert n_slab == 4 and n_out == 3 and n_blk & (n_blk - 1) == 0 and n_blk >= 8 and slot_dev > 1
     bf16, f32 = amplitudes.dtype, jnp.float32
     piece = (slot_dev, row_part, tile_len)
     dma = pltpu.SemaphoreType.DMA
@@ -350,10 +426,11 @@
             pltpu.VMEM((3, padded, padded), bf16),
             pltpu.VMEM((blocks, blocks, tile_len, tile_len), f32),
             pltpu.VMEM((blocks, blocks, tile_len, tile_len), f32),
-            pltpu.VMEM((2, n_slab, n_z) + piece, f32),
-            pltpu.VMEM((3, n_slab, n_z) + piece, f32),
-            pltpu.VMEM((3, 2, 2, half_z) + piece, f32),
-            pltpu.VMEM((3, 2, half_z) + piece, f32),
+            pltpu.VMEM((2, 2, 2, n_z // 2, 2) + piece, f32),
+            pltpu.VMEM((3, 2, 2, n_z // 2, 2) + piece, f32),
+            pltpu.VMEM((3, 2, 2, n_z // 2) + piece, f32),
+            pltpu.VMEM((3, 2, 2, half_hi, 2) + piece, f32),
+            pltpu.VMEM((3, 2, half_hi, 2) + piece, f32),
             pltpu.VMEM((3, n_z) + piece, f32),
             dma((2,)),
             dma((3,)),
@@ -361,12 +438,14 @@
             dma((3, n_blk)),
             dma((3, 4)),
             dma((3, 4)),
-            dma((3, 2, 2)),
-            dma((3, 2, 2)),
-            dma((3, 2)),
-            dma((3, 2)),
-            dma((3, n_z)),
-            dma((3, n_z)),
+            dma((n_jobs, 4)),
+            dma((n_jobs, 4)),
+            dma((n_jobs, 2, 2)),
+            dma((n_jobs, 2, 2)),
+            dma((n_jobs, 2)),
+            dma((n_jobs, 2)),
+            dma((n_jobs, n_z)),
+            dma((n_jobs, n_z)),
         ],
         compiler_params=pltpu.CompilerParams(
             collective_id=0, has_side_effects=True, vmem_limit_bytes=67043328

time: 183 us -> 174 us (0.951)
  Pallas kernels: 179 us -> 171 us
    pallas_call x1, Pallas kernels: 179 us -> 171 us  [local(): pl.pallas_call(functools.partial(cycle_kernel, dims), out_shape=jax.Shape...]
where the time goes in v3:
time: 174 us
  Pallas kernels  171 us (98%)
    pallas_call x1, Pallas kernels, local(): pl.pallas_call(functools.partial(cycle_kernel, dims), out_shape=jax.Shape...  171 us

profile of v3, /device:TPU:0, one launch (start us, length us, event | category | flops | bytes accessed | tf_op | source)
XLA Modules:
  0.0 174.0 jit_solution(15321762669176790306)
XLA Ops:
  0.0 1.3 select_reduce_fusion.of_ref
  1.3 171.0 %cycle.1 = f32[3,7,32,128]{3,2,1,0:T(8,128)} custom-call(s32[100]{0:T(128)} %select_reduce_fusion.of_ref, s32[56]{0:T(128)} %slot_ref.1, bf16[8,3,7,128,128]{4,3,2,1,0:T(8,128)(2,1)} %amp_ref.1, bf16[1,3,1200,1200]{3,2,1,0:T(8,128)(2,1)} %int_ref.1), custom_call_target="tpu_custom_call" | custom-call | tf_op jit(solution)/shard_map/cycle/pallas_call | solution.py:412
  172.3 1.7 copy.5

commit v4 on v3

--- a/solution.py
+++ b/solution.py
@@ -20,10 +20,6 @@
             out = out + bit * (1 - 2 * ((index // bit) % 2))
         bit *= 2
     return out
-
-
-def plain_places(slot_dev):
-    return max(1, slot_dev * 5 // 7), max(1, slot_dev * 5 // 7)
 
 
 def row_chunk(rows):
@@ -41,15 +37,16 @@
     n_slab, n_blk, blocks, v_width, slot_dev, tile_len = dims
     n_z = n_blk // 2
     padded = blocks * tile_len
-    cut = plain_places(slot_dev)
+    c0, c1, c2 = (max(1, slot_dev * c // 7) for c in (4, 3, 5))
     jobs = (
         (0, pl.ds(0, slot_dev), False),
-        (1, pl.ds(0, cut[0]), False),
-        (1, pl.ds(cut[0], slot_dev - cut[0]), True),
-        (2, pl.ds(0, cut[1]), False),
-        (2, pl.ds(cut[1], slot_dev - cut[1]), True),
+        (1, pl.ds(0, c0), False),
+        (1, pl.ds(c0, slot_dev - c0), True),
+        (2, pl.ds(0, c1), False),
+        (2, pl.ds(c1, c2 - c1), False),
+        (2, pl.ds(c2, slot_dev - c2), True),
     )
-    whole01, plain02, low02, plain12, low12 = range(5)
+    whole01, plain02, low02, plain12, more12, low12 = range(6)
     row_part = tile_len // n_slab
     n_slots = n_blk * slot_dev
     packed = (packed0, packed1, packed2)
@@ -215,6 +212,9 @@
             device_id_type=MESH,
         )
 
+    def held(job):
+        return jobs[job][1].size > 0
+
     def low_copy(job, mask):
         pair, places, _ = jobs[job]
         p_y, p_x = part_of(mask)
@@ -272,6 +272,8 @@
         )
 
     def first_start(job, mask):
+        if not held(job):
+            return
         if mask == 3:
             first_copy(job, 0, 1).start()
             first_copy(job, 1, 1).start()
@@ -286,12 +288,14 @@
             for job, (owner, _, low) in enumerate(jobs):
                 if owner == pair and low:
                     low_copy(job, mask).start()
-                elif owner == pair:
+                elif owner == pair and job != more12:
                     first_start(job, mask)
         for mask in PARTS:
             mate_copy(pair, mask).wait_send()
 
     def low_finish(job):
+        if not held(job):
+            return
         pair, places, _ = jobs[job]
         for mask in PARTS:
             low_copy(job, mask).wait_recv()
@@ -302,6 +306,8 @@
             first_start(job, mask)
 
     def first_finish(job):
+        if not held(job):
+            return
         pair, places, _ = jobs[job]
         for half in (0, 1):
             at = (pair, *part_of(2 if half == 0 else 1), halves[half], z_range(job), places)
@@ -310,6 +316,8 @@
             second_copy(job, half).start()
 
     def second_finish(job):
+        if not held(job):
+            return
         pair, places, _ = jobs[job]
         for half in (0, 1):
             at = (pair, s_y, s_x, halves[half], z_range(job), places)
@@ -322,10 +330,14 @@
             )
 
     def last_start(job):
+        if not held(job):
+            return
         for mask in last_masks(job):
             last_copy(job, mask).start()
 
     def last_finish(job):
+        if not held(job):
+            return
         pair, places, _ = jobs[job]
         total = mates[pair, s_y, s_x, z_hi, z_lo, places]
         for mask in last_masks(job):
@@ -356,28 +368,39 @@
     by_columns(acc_a, False, ((-1, 2, 1),), EARLY)
     first_finish(plain02)
     pack(acc_a, pair12)
+    mates_finish(pair12)
     low_finish(low02)
-    mates_finish(pair12)
     second_finish(plain02)
     last_start(plain02)
+    first_finish(plain12)
+    for mask in PARTS:
+        first_start(more12, mask)
     first_finish(low02)
-    first_finish(plain12)
+    low_finish(low12)
+    second_finish(plain12)
+    last_start(plain12)
+    first_finish(more12)
     second_finish(low02)
     last_start(low02)
-    low_finish(low12)
     first_finish(low12)
-    second_finish(plain12)
-    last_start(plain12)
+    second_finish(more12)
+    last_start(more12)
     second_finish(low12)
     last_start(low12)
-    for job in range(len(jobs)):
-        last_finish(job)
+    last_finish(whole01)
+    last_finish(plain02)
+    last_finish(low02)
+    last_finish(plain12)
+    last_finish(more12)
+    last_finish(low12)
 
     for mask in order:
         amp_copy(0, mask).wait_send()
         amp_copy(1, mask).wait_send()
         amp_copy(2, mask).wait_send()
     for job, (_, _, low) in enumerate(jobs):
+        if not held(job):
+            continue
         for mask in PARTS:
             if low:
                 low_copy(job, mask).wait_send()
@@ -399,7 +422,7 @@
     row_part = tile_len // n_slab
     n_z = n_blk // 2
     half_hi = n_z // 4
-    n_jobs = 5
+    n_jobs = 6
     assert n_slab == 4 and n_out == 3 and n_blk & (n_blk - 1) == 0 and n_blk >= 8 and slot_dev > 1
     bf16, f32 = amplitudes.dtype, jnp.float32
     piece = (slot_dev, row_part, tile_len)

time: 174 us -> 173 us (level)
  no operation moved by 1% of the time
where the time goes in v4:
time: 173 us
  Pallas kernels  170 us (98%)
  local copies, waits for them, and re-layouts  1.73 us (1%)
    pallas_call x1, Pallas kernels, local(): pl.pallas_call(functools.partial(cycle_kernel, dims), out_shape=jax.Shape...  170 us

profile of v4, /device:TPU:0, one launch (start us, length us, event | category | flops | bytes accessed | tf_op | source)
XLA Modules:
  0.0 173.0 jit_solution(5413717433652035730)
XLA Ops:
  0.0 1.3 select_reduce_fusion.of_ref
  1.3 170.0 %cycle.1 = f32[3,7,32,128]{3,2,1,0:T(8,128)} custom-call(s32[100]{0:T(128)} %select_reduce_fusion.of_ref, s32[56]{0:T(128)} %slot_ref.1, bf16[8,3,7,128,128]{4,3,2,1,0:T(8,128)(2,1)} %amp_ref.1, bf16[1,3,1200,1200]{3,2,1,0:T(8,128)(2,1)} %int_ref.1), custom_call_target="tpu_custom_call" | custom-call | tf_op jit(solution)/shard_map/cycle/pallas_call | solution.py:435
  171.2 1.7 %copy.5 = f32[3,7,32,128]{3,2,1,0:T(8,128)} copy(f32[3,7,32,128]{3,2,1,0:T(8,128)} %cycle.1) | data formatting | bytes 688128
